TPU v7x, 32 devices: a whole 2x2x4 slice. The times are simulated.
32 devices in a mesh: grp: 2 (over core), shard: 16 (over z, y, x).
Axes of the slice: x: 2, y: 2, z: 4, core: 2. Of those that a mesh axis runs over, the one named last changes fastest.
Arguments:
- blocks: float32 [2048, 128, 128], P(('grp', 'shard')), may hold values from -0.1875 to 0.1875
- block_row: int32 [2048], P(('grp', 'shard')), may hold values from 0 to 511, as said below
- block_owner: int32 [2048, 1], P(('grp', 'shard')), may hold values from 0 to 15; in each aligned block of 64 rows (0 to 63, 64 to 127, ...) at most 8 rows name the same one
- block_col: int32 [2048], P(('grp', 'shard')), may hold values from 0 to 15
- right_side: float32 [65536, 8], P(('grp', 'shard')), may hold values from -6 to 6
Outputs:
- solution: float32 [32768, 8], P('shard')
- left_vector: float32 [65536, 8], P(('grp', 'shard'))
- rel_residual: float32 [8], replicated
Inputs may be any that keep to these rules, and one draw needn't show every extreme that they name: `block_row`: block k lies in a row block of the device that holds it: between (k // 64) * 16 and (k // 64) * 16 + 15. `block_owner`: among the 64 blocks of one device, each owner is named at most 8 times, and in every draw some device names some owner exactly 8 times. `block_col`: a column block index among the 16 of the owner.
All inputs are finite; a program needn't handle non-finite values.
Results may differ from a plain program's by a relative error of at most 0.00024.
Values sent between devices are 32-bit elements; how exact they have to be, the bound alone decides.
A program may use at most 64 MiB of HBM per device.

v0:
```python
import jax
import jax.numpy as jnp
from jax import lax
from jax.sharding import PartitionSpec as P

ITERS = 4
COLS_OWN = 16


PRECISE = lax.Precision.HIGHEST


def squares_by_column(values):
    return jnp.sum(values * values, axis=0)


def rotate(state, norm_left, norm_right, right_vec):
    solution, search, diag_bar, residual_norm = state
    radius = jnp.sqrt(diag_bar * diag_bar + norm_left * norm_left)
    cosine = diag_bar / radius
    sine_term = norm_left / radius
    coupling = sine_term * norm_right
    step_size = cosine * residual_norm
    solution = solution + step_size / radius * search
    search = right_vec - coupling / radius * search
    return (solution, search, -cosine * norm_right, sine_term * residual_norm)


def on_device(blocks, block_row, block_owner, block_col, right_side):
    count = blocks.shape[0]
    block_width = blocks.shape[1]
    columns = right_side.shape[1]
    flat_width = block_width * columns
    owners = lax.axis_size("shard")
    capacity = 2 * count // owners
    row_blocks = right_side.shape[0] // block_width
    first_row = lax.axis_index(("grp", "shard")) * row_blocks
    local_row = block_row - first_row
    row_onehot = (local_row[:, None] == jnp.arange(row_blocks, dtype=jnp.int32)[None, :]).astype(
        jnp.float32
    )
    owner = block_owner[:, 0]
    owner_onehot = (owner[:, None] == jnp.arange(owners, dtype=jnp.int32)[None, :]).astype(
        jnp.int32
    )
    earlier = jnp.cumsum(owner_onehot, axis=0) - owner_onehot
    slot_rank = jnp.sum(earlier * owner_onehot, axis=1)
    position = owner * capacity + slot_rank
    source = (
        jnp.full((owners * capacity,), count, jnp.int32)
        .at[position]
        .set(jnp.arange(count, dtype=jnp.int32))
    )
    sent_cols = jnp.concatenate([block_col, jnp.full((1,), -1, jnp.int32)])[source]
    got_cols = lax.all_to_all(sent_cols, "shard", split_axis=0, concat_axis=0, tiled=True)
    col_onehot = (got_cols[:, None] == jnp.arange(COLS_OWN, dtype=jnp.int32)[None, :]).astype(
        jnp.float32
    )

    def adjoint(vector):
        pieces = vector.reshape(row_blocks, block_width, columns)[local_row]
        product = jnp.einsum("kij,kir->kjr", blocks, pieces, precision=PRECISE).reshape(
            count, flat_width
        )
        padded = jnp.concatenate([product, jnp.zeros((1, flat_width), jnp.float32)])
        incoming = lax.all_to_all(padded[source], "shard", split_axis=0, concat_axis=0, tiled=True)
        owned = jnp.dot(col_onehot.T, incoming, precision=PRECISE)
        owned = lax.psum(owned, "grp")
        return owned.reshape(COLS_OWN * block_width, columns)

    def norm_rows(values):
        return jnp.sqrt(lax.psum(squares_by_column(values), ("grp", "shard")))

    def norm_columns(values):
        return jnp.sqrt(lax.psum(squares_by_column(values), "shard"))

    norm_start = norm_rows(right_side)
    left_vec = right_side / norm_start
    right_raw = adjoint(left_vec)
    norm_left = norm_start
    for repeat in range(ITERS):
        flat = right_raw.reshape(COLS_OWN, flat_width)
        outgoing = jnp.dot(col_onehot, flat, precision=PRECISE)
        forward_incoming = lax.all_to_all(
            outgoing, "shard", split_axis=0, concat_axis=0, tiled=True
        )
        forward_pieces = forward_incoming[position]
        forward_pieces = forward_pieces.reshape(count, block_width, columns)
        forward_product = jnp.einsum("kij,kjr->kir", blocks, forward_pieces, precision=PRECISE)
        summed = jnp.dot(
            row_onehot.T, forward_product.reshape(count, flat_width), precision=PRECISE
        )
        image = summed.reshape(row_blocks * block_width, columns)
        norm_right = norm_columns(right_raw)
        right_vec = right_raw / norm_right
        if repeat == 0:
            state = (jnp.zeros_like(right_vec), right_vec, norm_right, norm_start)
        else:
            state = rotate(state, norm_left, norm_right, right_vec)
        left_raw = image / norm_right - norm_right * left_vec
        terms = adjoint(left_raw)
        norm_left = norm_rows(left_raw)
        left_vec = left_raw / norm_left
        right_raw = terms / norm_left - norm_left * right_vec
    norm_right = norm_columns(right_raw)
    right_vec = right_raw / norm_right
    state = rotate(state, norm_left, norm_right, right_vec)
    return (state[0], left_vec, state[3] / norm_start)


def solution(mesh):
    placed = (
        P(("grp", "shard"), None, None),
        P(("grp", "shard")),
        P(("grp", "shard"), None),
        P(("grp", "shard")),
        P(("grp", "shard"), None),
    )
    return jax.shard_map(
        on_device,
        mesh=mesh,
        in_specs=placed,
        out_specs=(P("shard", None), P(("grp", "shard"), None), P()),
        check_vma=False,
    )
```

profile of v0, /device:TPU:0, one launch (start us, length us, event | category | flops | bytes accessed | tf_op | source)
XLA Modules:
  0.0 590.9 jit_solution(7024942218735535955)
XLA Ops:
  13.0 8.3 %all-to-all-start = ((s32[16,8,1]{1,2,0:T(1,128)}), s32[16,8,1]{1,2,0:T(1,128)S(1)}, u32[]{:S(2)}, u32[]{:S(2)}) async-start(s32[16,8,1]{1,2,0:T(1,128)} %bitcast.3), calls=%async_computation | async-start | bytes 16384 | tf_op jit(solution)/shard_map/all_to_all | solution.py:55
  22.3 40.6 %psum.91 = f32[8]{0:T(128)S(1)} all-reduce(f32[8]{0:T(128)S(1)} %multiply_reduce_fusion.8), channel_id=1, replica_groups=mesh['grp'=2,'shard'=16] {'grp','shard'}, use_global_device_ids=true, to_apply=%region_4.5 | all-reduce | flops 8 | bytes 64 | tf_op jit(solution)/shard_map/psum | solution.py:72
  72.5 5.5 all-to-all-start.1
  79.3 13.0 %all-to-all-done.1 = f32[16,8,1024]{2,1,0:T(8,128)S(1)} async-done(((f32[16,8,1024]{2,1,0:T(8,128)}), f32[16,8,1024]{2,1,0:T(8,128)S(1)}, u32[]{:S(2)}, u32[]{:S(2)}) %all-to-all-start.1) | async-done | bytes 524320 | tf_op jit(solution)/shard_map/all_to_all | solution.py:66
  93.4 16.1 %all-reduce.9.cloned.1.call-done = f32[16,1024]{1,0:T(8,128)} async-done(((f32[16,1024]{1,0:T(8,128)}), f32[16,1024]{1,0:T(8,128)}) %all-reduce.9.cloned.1.call-update) | async-done | bytes 65552 | tf_op jit(solution)/shard_map/psum | solution.py:68
  111.5 6.8 %all-to-all-start.2 = ((f32[16,8,1024]{2,1,0:T(8,128)}), f32[16,8,1024]{2,1,0:T(8,128)S(1)}, u32[]{:S(2)}, u32[]{:S(2)}) async-start(f32[16,8,1024]{2,1,0:T(8,128)} %convolution_bitcast_fusion), calls=%async_computation.2 | async-start | bytes 1048576 | tf_op jit(solution)/shard_map/all_to_all | solution.py:84
  120.1 42.5 %psum.93 = f32[8]{0:T(128)S(1)} all-reduce(f32[8]{0:T(128)S(1)} %multiply_reduce_fusion), channel_id=1, replica_groups=mesh['grp'=2,'shard'=16] {'shard'}, use_global_device_ids=true, to_apply=%region_7.8 | all-reduce | flops 8 | bytes 64 | tf_op jit(solution)/shard_map/psum | solution.py:75
  163.7 8.4 %convolution_bitcast_fusion.7 = f32[64,128,8]{1,2,0:T(8,128)S(1)} fusion(f32[64,128,8]{1,2,0:T(8,128)S(1)} %copy.106, f32[64,128,128]{2,1,0:T(8,128)} %param.5), kind=kOutput, calls=%fused_computation.21 | convolution fusion | flops 100663296 | bytes 4718592 | tf_op jit(solution)/shard_map/kij,kjr->kir/dot_general | solution.py:89
  181.1 13.4 %all_to_all.96 = f32[16,8,1024]{2,1,0:T(8,128)S(1)} all-to-all(f32[16,8,1024]{2,1,0:T(8,128)S(1)} %bitcast.108), channel_id=1, replica_groups=mesh['grp'=2,'shard'=16] {'shard'}, dimensions={0} | all-to-all | bytes 1048576 | tf_op jit(solution)/shard_map/all_to_all | solution.py:66
  195.6 38.8 %psum.94 = f32[8]{0:T(128)S(1)} all-reduce(f32[8]{0:T(128)S(1)} %get-tuple-element.32), channel_id=1, replica_groups=mesh['grp'=2,'shard'=16] {'grp','shard'}, use_global_device_ids=true, to_apply=%region_9.10 | all-reduce | flops 8 | bytes 64 | tf_op jit(solution)/shard_map/psum | solution.py:72
  236.6 5.3 all-to-all-start.4
  244.2 42.6 %psum.96 = f32[8]{0:T(128)S(1)} all-reduce(f32[8]{0:T(128)S(1)} %get-tuple-element.30), channel_id=1, replica_groups=mesh['grp'=2,'shard'=16] {'shard'}, use_global_device_ids=true, to_apply=%region_12.13 | all-reduce | flops 8 | bytes 64 | tf_op jit(solution)/shard_map/psum | solution.py:75
  288.0 8.3 %convolution_bitcast_fusion.5 = f32[64,128,8]{1,2,0:T(8,128)S(1)} fusion(f32[64,128,8]{1,2,0:T(8,128)S(1)} %copy.116, f32[64,128,128]{2,1,0:T(8,128)} %param.5), kind=kOutput, calls=%fused_computation.19 | convolution fusion | flops 100663296 | bytes 4718592 | tf_op jit(solution)/shard_map/kij,kjr->kir/dot_general | solution.py:89
  305.3 13.4 %all_to_all.97 = f32[16,8,1024]{2,1,0:T(8,128)S(1)} all-to-all(f32[16,8,1024]{2,1,0:T(8,128)S(1)} %bitcast.109), channel_id=1, replica_groups=mesh['grp'=2,'shard'=16] {'shard'}, dimensions={0} | all-to-all | bytes 1048576 | tf_op jit(solution)/shard_map/all_to_all | solution.py:66
  319.8 38.8 %psum.97 = f32[8]{0:T(128)S(1)} all-reduce(f32[8]{0:T(128)S(1)} %get-tuple-element.28), channel_id=1, replica_groups=mesh['grp'=2,'shard'=16] {'grp','shard'}, use_global_device_ids=true, to_apply=%region_14.15 | all-reduce | flops 8 | bytes 64 | tf_op jit(solution)/shard_map/psum | solution.py:72
  360.8 5.3 all-to-all-start.6
  368.1 42.3 %psum.99 = f32[8]{0:T(128)S(1)} all-reduce(f32[8]{0:T(128)S(1)} %get-tuple-element.26), channel_id=1, replica_groups=mesh['grp'=2,'shard'=16] {'shard'}, use_global_device_ids=true, to_apply=%region_17.18 | all-reduce | flops 8 | bytes 64 | tf_op jit(solution)/shard_map/psum | solution.py:75
  411.5 8.3 %convolution_bitcast_fusion.3 = f32[64,128,8]{1,2,0:T(8,128)S(1)} fusion(f32[64,128,8]{1,2,0:T(8,128)S(1)} %copy.123, f32[64,128,128]{2,1,0:T(8,128)} %param.5), kind=kOutput, calls=%fused_computation.17 | convolution fusion | flops 100663296 | bytes 4718592 | tf_op jit(solution)/shard_map/kij,kjr->kir/dot_general | solution.py:89
  428.9 13.4 %all_to_all.98 = f32[16,8,1024]{2,1,0:T(8,128)S(1)} all-to-all(f32[16,8,1024]{2,1,0:T(8,128)S(1)} %bitcast.107), channel_id=1, replica_groups=mesh['grp'=2,'shard'=16] {'shard'}, dimensions={0} | all-to-all | bytes 1048576 | tf_op jit(solution)/shard_map/all_to_all | solution.py:66
  443.4 38.8 %psum.100 = f32[8]{0:T(128)S(1)} all-reduce(f32[8]{0:T(128)S(1)} %get-tuple-element.24), channel_id=1, replica_groups=mesh['grp'=2,'shard'=16] {'grp','shard'}, use_global_device_ids=true, to_apply=%region_19.20 | all-reduce | flops 8 | bytes 64 | tf_op jit(solution)/shard_map/psum | solution.py:72
  484.3 5.3 all-to-all-start.8
  491.6 42.3 %psum.102 = f32[8]{0:T(128)S(1)} all-reduce(f32[8]{0:T(128)S(1)} %get-tuple-element.22), channel_id=1, replica_groups=mesh['grp'=2,'shard'=16] {'shard'}, use_global_device_ids=true, to_apply=%region_22.23 | all-reduce | flops 8 | bytes 64 | tf_op jit(solution)/shard_map/psum | solution.py:75
  535.1 8.3 %convolution_bitcast_fusion.1 = f32[64,128,8]{1,2,0:T(8,128)S(1)} fusion(f32[64,128,8]{1,2,0:T(8,128)S(1)} %copy.130, f32[64,128,128]{2,1,0:T(8,128)} %param.5), kind=kOutput, calls=%fused_computation.15 | convolution fusion | flops 100663296 | bytes 4718592 | tf_op jit(solution)/shard_map/kij,kjr->kir/dot_general | solution.py:89
  545.2 36.9 %psum.103 = f32[8]{0:T(128)S(1)} all-reduce(f32[8]{0:T(128)S(1)} %get-tuple-element.20), channel_id=1, replica_groups=mesh['grp'=2,'shard'=16] {'grp','shard'}, use_global_device_ids=true, to_apply=%region_24.25 | all-reduce | flops 8 | bytes 64 | tf_op jit(solution)/shard_map/psum | solution.py:72
  (143 shorter events, 73.6 us)
Async XLA Ops:
  13.0 59.5 %all-to-all-start = ((s32[16,8,1]{1,2,0:T(1,128)}), s32[16,8,1]{1,2,0:T(1,128)S(1)}, u32[]{:S(2)}, u32[]{:S(2)}) async-start(s32[16,8,1]{1,2,0:T(1,128)} %bitcast.3), calls=%async_computation | async-start | bytes 16384 | tf_op jit(solution)/shard_map/all_to_all | solution.py:55
  72.5 19.9 %all-to-all-start.1 = ((f32[16,8,1024]{2,1,0:T(8,128)}), f32[16,8,1024]{2,1,0:T(8,128)S(1)}, u32[]{:S(2)}, u32[]{:S(2)}) async-start(f32[16,8,1024]{2,1,0:T(8,128)} %bitcast.7), calls=%async_computation.1 | async-start | bytes 1048576 | tf_op jit(solution)/shard_map/all_to_all | solution.py:66
  78.0 31.5 %all-reduce.9.cloned.1.call-start = ((), (), s32[]{:S(2)}) async-start(), calls=%async_computation.9 | async-start | bytes 131072 | tf_op jit(solution)/shard_map/psum | solution.py:68
  111.5 51.1 %all-to-all-start.2 = ((f32[16,8,1024]{2,1,0:T(8,128)}), f32[16,8,1024]{2,1,0:T(8,128)S(1)}, u32[]{:S(2)}, u32[]{:S(2)}) async-start(f32[16,8,1024]{2,1,0:T(8,128)} %convolution_bitcast_fusion), calls=%async_computation.2 | async-start | bytes 1048576 | tf_op jit(solution)/shard_map/all_to_all | solution.py:84
  118.3 116.2 %all-reduce.11.cloned.1.call-start = ((), (), s32[]{:S(2)}) async-start(), calls=%async_computation.10 | async-start | bytes 131072 | tf_op jit(solution)/shard_map/psum | solution.py:68
  163.7 10.0 %copy-start = (f32[2048,8]{0,1:T(8,128)S(1)}, f32[2048,8]{0,1:T(8,128)}, u32[]{:S(2)}) copy-start(f32[2048,8]{0,1:T(8,128)} %param.9) | copy-start | bytes 196612
  180.1 54.4 %copy-start.1 = (f32[16,1024]{1,0:T(8,128)S(1)}, f32[16,1024]{1,0:T(8,128)}, u32[]{:S(2)}) copy-start(f32[16,1024]{1,0:T(8,128)} %all-reduce.9.cloned.1.call-done) | copy-start | bytes 196612
  236.6 50.3 %all-to-all-start.4 = ((f32[16,8,1024]{2,1,0:T(8,128)}), f32[16,8,1024]{2,1,0:T(8,128)S(1)}, u32[]{:S(2)}, u32[]{:S(2)}) async-start(f32[16,8,1024]{2,1,0:T(8,128)} %fusion.20), calls=%async_computation.4 | async-start | bytes 1048576 | tf_op jit(solution)/shard_map/all_to_all | solution.py:84
  241.9 116.8 %all-reduce.13.cloned.1.call-start = ((), (), s32[]{:S(2)}) async-start(), calls=%async_computation.11 | async-start | bytes 131072 | tf_op jit(solution)/shard_map/psum | solution.py:68
  304.3 54.4 %copy-start.2 = (f32[16,1024]{1,0:T(8,128)S(1)}, f32[16,1024]{1,0:T(8,128)}, u32[]{:S(2)}) copy-start(f32[16,1024]{1,0:T(8,128)} %all-reduce.11.cloned.1.call-done) | copy-start | bytes 196612
  360.8 49.6 %all-to-all-start.6 = ((f32[16,8,1024]{2,1,0:T(8,128)}), f32[16,8,1024]{2,1,0:T(8,128)S(1)}, u32[]{:S(2)}, u32[]{:S(2)}) async-start(f32[16,8,1024]{2,1,0:T(8,128)} %fusion.18), calls=%async_computation.6 | async-start | bytes 1048576 | tf_op jit(solution)/shard_map/all_to_all | solution.py:84
  366.1 116.2 %all-reduce.15.cloned.1.call-start = ((), (), s32[]{:S(2)}) async-start(), calls=%async_computation.12 | async-start | bytes 131072 | tf_op jit(solution)/shard_map/psum | solution.py:68
  427.9 54.4 %copy-start.3 = (f32[16,1024]{1,0:T(8,128)S(1)}, f32[16,1024]{1,0:T(8,128)}, u32[]{:S(2)}) copy-start(f32[16,1024]{1,0:T(8,128)} %all-reduce.13.cloned.1.call-done) | copy-start | bytes 196612
  484.3 49.6 %all-to-all-start.8 = ((f32[16,8,1024]{2,1,0:T(8,128)}), f32[16,8,1024]{2,1,0:T(8,128)S(1)}, u32[]{:S(2)}, u32[]{:S(2)}) async-start(f32[16,8,1024]{2,1,0:T(8,128)} %fusion.16), calls=%async_computation.8 | async-start | bytes 1048576 | tf_op jit(solution)/shard_map/all_to_all | solution.py:84
Sparse Core Ops, SparseCore 0:
  93.5 15.9 all-reduce.8
  195.6 16.0 all-reduce.10
  319.8 16.0 all-reduce.12
  443.4 16.0 all-reduce.14
where the time goes:
time: 598 us; the launch traced here: 591 us
  blocking collectives  404 us (68%)
  matrix products  68.2 us (11%)
  starting transfers between devices  36.9 us (6%)
  waiting for transfers between devices  29.3 us (5%)
  local copies, waits for them, and re-layouts  28.3 us (5%)
  between operations  14.6 us (2%)
  other arithmetic  10.2 us (2%)
    psum x5, blocking collectives, norm_rows(): return jnp.sqrt(lax.psum(squares_by_column(values), ('grp', 'shard')))  194 us
    psum x4, blocking collectives, norm_columns(): return jnp.sqrt(lax.psum(squares_by_column(values), 'shard'))  170 us
    all_to_all x3, blocking collectives, adjoint(): lax.all_to_all(padded[source], 'shard', split_axis=0, concat_axis=0, tile...  40.2 us
    dot_general x4, matrix products, on_device(): jnp.einsum('kij,kjr->kir', blocks, forward_pieces, precision=PRECISE)  33.3 us
    all_to_all x4, starting transfers between devices, on_device(): lax.all_to_all(outgoing, 'shard', split_axis=0, concat_axis=0, tiled=True)  22.9 us
    dot_general x4, matrix products, adjoint(): jnp.einsum('kij,kir->kjr', blocks, pieces, precision=PRECISE)  21.2 us
    psum x4, waiting for transfers between devices, adjoint(): owned = lax.psum(owned, 'grp')  16.2 us
    all_to_all x1, waiting for transfers between devices, adjoint(): lax.all_to_all(padded[source], 'shard', split_axis=0, concat_axis=0, tile...  13 us
  transfers between devices with their start and end apart: 10, of which 2 were waited for; matrix products, arithmetic and copies ran while one was open for 3% of the time, Pallas kernels for 0%

commit v1 on v0

v1 whole, which is shorter than its diff:
```python
import functools

import jax
import jax.numpy as jnp
from jax import lax
from jax.experimental import pallas as pl
from jax.experimental.pallas import tpu as pltpu
from jax.sharding import PartitionSpec as P

ITERS = 4
COLS_OWN = 16
HALF = COLS_OWN // 2
PLANE = 4
LOADS = 8
MESH = pl.DeviceIdType.MESH
F32 = jnp.float32
BF16 = jnp.bfloat16


def split(value):
    high = value.astype(BF16).astype(F32)
    return high, value - high


def total(tile):
    return jnp.broadcast_to(jnp.sum(tile, axis=-1, keepdims=True), tile.shape)


def kernel(
    shards, count, rows,
    owner_ref, col_ref, row_ref, code_ref, blocks_ref, right_ref,
    sol_ref, left_out, rel_ref,
    raw, pair, scatter, gather_rows, prod, left, unit, image,
    full, part, cross, from_a, from_b, relay, from_z, to_z, norms, norms_in,
    own, search, bidiag,
    load_sem, x_send, x_recv, a_send, a_recv, b_send, b_recv, c_send, c_recv,
    z_send, z_recv, p_send, p_recv, g_send, g_recv, n_send, n_recv,
):
    line = shards // PLANE
    grp = lax.axis_index("grp")
    me = lax.axis_index("shard")
    high, low = me // PLANE, me % PLANE

    def flip(d):
        bit0 = low % 2
        bit1 = low // 2
        if d & 1:
            bit0 = 1 - bit0
        if d & 2:
            bit1 = 1 - bit1
        return bit1 * 2 + bit0

    lows = [flip(d) for d in range(PLANE)]
    ahead = [lax.rem(high + e, line) for e in range(line)]
    behind = [lax.rem(high + line - e, line) for e in range(line)]
    partner = (1 - grp, me)
    plane = {d: (grp, high * PLANE + lows[d]) for d in (1, 2)}
    along = {e: (grp, ahead[e] * PLANE + low) for e in range(1, line)}

    def remote(src, dst, send, recv, device):
        return pltpu.make_async_remote_copy(
            src_ref=src, dst_ref=dst, send_sem=send, recv_sem=recv,
            device_id=device, device_id_type=MESH,
        )

    per_load = count // LOADS
    loads = [
        pltpu.make_async_copy(
            blocks_ref.at[pl.ds(i * per_load, per_load)],
            raw.at[pl.ds(i * per_load, per_load)],
            load_sem.at[i],
        )
        for i in range(LOADS)
    ]
    for copy in loads:
        copy.start()

    barrier = pltpu.get_barrier_semaphore()
    greeted = [partner, plane[1], plane[2]] + [along[e] for e in range(1, line)]
    for device in greeted:
        pl.semaphore_signal(barrier, inc=1, device_id=device, device_id_type=MESH)

    squares = jnp.zeros((8, 128), F32)
    for r in range(rows):
        tile = right_ref[:, r * 128:(r + 1) * 128]
        left[r] = tile
        squares = squares + tile * tile
    norms[0] = squares

    codes = code_ref[0:1, :]
    row_codes = code_ref[1:2, :]
    ids = lax.broadcasted_iota(jnp.int32, (HALF * 8, count * 8), 0)

    def build(q, carry):
        scatter[q] = jnp.where(ids + q * (HALF * 8) == codes, 1.0, 0.0).astype(BF16)
        return carry

    lax.fori_loop(0, 2 * shards, build, 0)
    row_ids = lax.broadcasted_iota(jnp.int32, (rows * 8, count * 8), 0)
    gather_rows[...] = jnp.where(row_ids == row_codes, 1.0, 0.0).astype(BF16)

    for i, copy in enumerate(loads):
        copy.wait()

        def narrow(k, carry):
            block = raw[k]
            upper = block.astype(BF16)
            pair[k, :, 0:128] = upper
            pair[k, :, 128:256] = (block - upper.astype(F32)).astype(BF16)
            return carry

        lax.fori_loop(i * per_load, (i + 1) * per_load, narrow, 0, unroll=2)

    for j in range(COLS_OWN):
        own[j] = jnp.zeros((8, 128), F32)
        search[j] = jnp.zeros((8, 128), F32)
        sol_ref[:, j * 128:(j + 1) * 128] = jnp.zeros((8, 128), F32)

    pl.semaphore_wait(barrier, len(greeted))

    def both(tile):
        upper, lower = split(tile)
        return jnp.concatenate([upper, lower], axis=0).astype(BF16)

    def store_products(step, tiles):
        merged = jnp.concatenate(tiles, axis=0)
        upper, lower = split(merged)
        start = pl.multiple_of(step * 8 * len(tiles), 16)
        prod[pl.ds(start, 8 * len(tiles)), 0:128] = upper.astype(BF16)
        prod[pl.ds(start, 8 * len(tiles)), 128:256] = lower.astype(BF16)

    def adjoint(step, carry):
        tiles = []
        for i in range(4):
            k = step * 4 + i
            out = jnp.dot(both(left[row_ref[k] % rows]), pair[k], preferred_element_type=F32)
            out = out[:, 0:128] + out[:, 128:256]
            tiles.append(out[0:8] + out[8:16])
        store_products(step, tiles)
        return carry

    def forward(step, carry):
        tiles = []
        for i in range(4):
            k = step * 4 + i
            col = col_ref[k]
            tile = full[(col // HALF) * shards + owner_ref[k], col % HALF]
            lhs = both(tile)
            lhs = jnp.concatenate([lhs, lhs], axis=1)
            out = lax.dot_general(
                lhs, pair[k], (((1,), (1,)), ((), ())), preferred_element_type=F32
            )
            tiles.append(out[0:8] + out[8:16])
        store_products(step, tiles)
        return carry

    def columns_of(half):
        for c in range(shards // 16):
            base = half * shards + c * 16
            lhs = scatter[pl.ds(base, 16)].reshape(16 * HALF * 8, count * 8)
            out = jnp.dot(lhs, prod[...], preferred_element_type=F32)
            out = out[:, 0:128] + out[:, 128:256]
            part[pl.ds(base, 16), 0:HALF] = out.reshape(16, HALF, 8, 128)
            part[pl.ds(base, 16), HALF] = jnp.broadcast_to(norms[0][None], (16, 8, 128))

    def reduce_scatter():
        sends = []
        columns_of(1 - grp)
        order = [e for e in range(1, line)] + [0]
        exchange = {}
        for e in order:
            first = ahead[e] * PLANE
            exchange[e] = remote(
                part.at[pl.ds((1 - grp) * shards + first, PLANE)],
                cross.at[pl.ds(first, PLANE)],
                x_send.at[e], x_recv.at[e], partner,
            )
            exchange[e].start()
        columns_of(grp)
        stage_a = {}
        for e in order:
            exchange[e].wait_recv()
            first = ahead[e] * PLANE
            cross[pl.ds(first, PLANE)] = (
                cross[pl.ds(first, PLANE)] + part[pl.ds(grp * shards + first, PLANE)]
            )
            a = 1 if e % 2 == 0 else 2
            for i, d in enumerate((3, a)):
                copy = remote(
                    cross.at[first + lows[d]], from_a.at[e, i],
                    a_send.at[e, i], a_recv.at[e, i], plane[a],
                )
                copy.start()
                stage_a[e, i] = copy
        stage_b = {}
        for e in order:
            first = ahead[e] * PLANE
            b = 2 if e % 2 == 0 else 1
            stage_a[e, 0].wait_recv()
            relay[e] = cross[first + lows[b]] + from_a[e, 0]
            stage_b[e] = remote(relay.at[e], from_b.at[e], b_send.at[e], b_recv.at[e], plane[b])
            stage_b[e].start()
        stage_c = {}
        for e in order:
            first = ahead[e] * PLANE
            stage_a[e, 1].wait_recv()
            mine = cross[first + low] + from_a[e, 1]
            stage_b[e].wait_recv()
            to_z[e] = mine + from_b[e]
            if e:
                stage_c[e] = remote(
                    to_z.at[e], from_z.at[e - 1], c_send.at[e - 1], c_recv.at[e - 1], along[e]
                )
                stage_c[e].start()
        for e in range(1, line):
            stage_c[e].wait_recv()
        summed = to_z[0]
        for e in range(1, line):
            summed = summed + from_z[e - 1]
        for copies in (exchange, stage_a, stage_b, stage_c):
            for copy in copies.values():
                copy.wait_send()
        return summed

    def slot(e, d):
        return grp * shards + behind[e] * PLANE + lows[d]

    def all_gather():
        sends = []

        def piece(e, d, send, recv, device):
            place = full.at[slot(e, d)]
            return remote(place, place, send, recv, device)

        for e in range(1, line):
            copy = piece(0, 0, z_send.at[e - 1], z_recv.at[e - 1], along[e])
            copy.start()
            sends.append(copy)

        def spread(e):
            for d in (1, 2):
                copy = piece(e, 0, p_send.at[d - 1, e], p_recv.at[d - 1, e], plane[d])
                copy.start()
                sends.append(copy)
            hand(e, 0)

        def hand(e, d):
            copy = piece(e, d, g_send.at[d, e], g_recv.at[d, e], partner)
            copy.start()
            sends.append(copy)

        def arrive(e, d):
            piece(e, d, p_send.at[d - 1, e], p_recv.at[d - 1, e], plane[1]).wait_recv()

        def pass_on(e):
            a = 1 if e % 2 == 0 else 2
            b = 3 - a
            arrive(e, a)
            copy = piece(e, a, p_send.at[2, e], p_recv.at[2, e], plane[b])
            copy.start()
            sends.append(copy)
            hand(e, a)
            arrive(e, b)
            hand(e, b)

        spread(0)
        for e in range(1, line):
            piece(e, 0, z_send.at[e - 1], z_recv.at[e - 1], along[e]).wait_recv()
            spread(e)
            pass_on(e - 1)
        pass_on(line - 1)
        for e in range(line):
            arrive(e, 3)
            hand(e, 3)
        other = (1 - grp) * shards
        for e in range(line):
            for d in range(PLANE):
                place = full.at[other + behind[e] * PLANE + lows[d]]
                remote(place, place, g_send.at[d, e], g_recv.at[d, e], partner).wait_recv()
        for copy in sends:
            copy.wait_send()

    def rotation(norm_left):
        diag_bar, residual = bidiag[0], bidiag[1]
        radius = jnp.sqrt(diag_bar * diag_bar + norm_left * norm_left)
        cosine = diag_bar / radius
        sine = norm_left / radius
        return radius, cosine, sine, residual

    def advance(radius, cosine, residual):
        step = cosine * residual / radius
        for j in range(COLS_OWN):
            place = slice(j * 128, (j + 1) * 128)
            sol_ref[:, place] = sol_ref[:, place] + step * search[j]

    bidiag[0] = jnp.ones((8, 128), F32)
    bidiag[1] = jnp.zeros((8, 128), F32)

    def iterate(it, carry):
        lax.fori_loop(0, count // 4, adjoint, 0)
        summed = reduce_scatter()
        norm_left = jnp.sqrt(total(summed[HALF]))
        squares = jnp.zeros((8, 128), F32)
        mine = slot(0, 0)
        previous = own[pl.ds(grp * HALF, HALF)]
        fresh = summed[0:HALF] / norm_left[None] - norm_left[None] * previous
        full[mine, 0:HALF] = fresh
        full[mine, HALF] = jnp.sum(fresh * fresh, axis=0)
        all_gather()
        norm_right = jnp.sqrt(total(jnp.sum(full[:, HALF], axis=0)))
        radius, cosine, sine, residual = rotation(norm_left)
        advance(radius, cosine, residual)
        shrink = sine * norm_right / radius
        for half in range(2):
            fresh = full[half * shards + me, 0:HALF] / norm_right[None]
            own[half * HALF:(half + 1) * HALF] = fresh
            search[half * HALF:(half + 1) * HALF] = (
                fresh - shrink[None] * search[half * HALF:(half + 1) * HALF]
            )
        bidiag[0] = jnp.where(it == 0, norm_right, -cosine * norm_right)
        bidiag[1] = jnp.where(it == 0, norm_left, sine * residual)
        bidiag[2] = jnp.where(it == 0, norm_left, bidiag[2])
        lax.fori_loop(0, count // 4, forward, 0)
        out = jnp.dot(gather_rows[...], prod[...], preferred_element_type=F32)
        out = (out[:, 0:128] + out[:, 128:256]).reshape(rows, 8, 128)
        fresh = out / norm_right[None] - norm_right[None] * (left[...] / norm_left[None])
        left[...] = fresh
        norms[0] = jnp.sum(fresh * fresh, axis=0)
        return carry

    bidiag[2] = jnp.zeros((8, 128), F32)
    lax.fori_loop(0, ITERS, iterate, 0)

    sent = []
    for i, device in enumerate((partner, plane[1], plane[2])):
        copy = remote(norms.at[i], norms_in.at[i], n_send.at[i], n_recv.at[i], device)
        copy.start()
        copy.wait_recv()
        norms[i + 1] = norms[i] + norms_in[i]
        sent.append(copy)
    summed = norms[3]
    for e in range(1, line):
        copy = remote(
            norms.at[3], norms_in.at[2 + e], n_send.at[2 + e], n_recv.at[2 + e], along[e]
        )
        copy.start()
        sent.append(copy)
    for e in range(1, line):
        sent[2 + e].wait_recv()
        summed = summed + norms_in[2 + e]
    norm_left = jnp.sqrt(total(summed))
    radius, cosine, sine, residual = rotation(norm_left)
    advance(radius, cosine, residual)
    for r in range(rows):
        left_out[:, r * 128:(r + 1) * 128] = left[r] / norm_left
    rel_ref[...] = sine * residual / bidiag[2]
    for copy in sent:
        copy.wait_send()


def on_device(blocks, block_row, block_owner, block_col, right_side):
    count = blocks.shape[0]
    rows = right_side.shape[0] // 128
    shards = lax.axis_size("shard")
    line = shards // PLANE
    owner = block_owner[:, 0]
    place = ((block_col // HALF) * shards + owner) * HALF + block_col % HALF
    both = jnp.stack([place, block_row % rows])
    codes = (both[:, :, None] * 8 + jnp.arange(8, dtype=jnp.int32)).reshape(2, count * 8)
    piece = (HALF + 1, 8, 128)
    smem = pl.BlockSpec(memory_space=pltpu.SMEM)
    vmem = pl.BlockSpec(memory_space=pltpu.VMEM)
    dma = pltpu.SemaphoreType.DMA
    sol, left, rel = pl.pallas_call(
        functools.partial(kernel, shards, count, rows),
        out_shape=(
            jax.ShapeDtypeStruct((8, COLS_OWN * 128), F32),
            jax.ShapeDtypeStruct((8, rows * 128), F32),
            jax.ShapeDtypeStruct((8, 128), F32),
        ),
        in_specs=[smem, smem, smem, vmem, pl.BlockSpec(memory_space=pl.ANY), vmem],
        out_specs=(vmem, vmem, vmem),
        scratch_shapes=[
            pltpu.VMEM((count, 128, 128), F32),
            pltpu.VMEM((count, 128, 256), BF16),
            pltpu.VMEM((2 * shards, HALF * 8, count * 8), BF16),
            pltpu.VMEM((rows * 8, count * 8), BF16),
            pltpu.VMEM((count * 8, 256), BF16),
            pltpu.VMEM((rows, 8, 128), F32),
            pltpu.VMEM((8, 128), F32),
            pltpu.VMEM((8, 128), F32),
            pltpu.VMEM((2 * shards,) + piece, F32),
            pltpu.VMEM((2 * shards,) + piece, F32),
            pltpu.VMEM((shards,) + piece, F32),
            pltpu.VMEM((line, 2) + piece, F32),
            pltpu.VMEM((line,) + piece, F32),
            pltpu.VMEM((line,) + piece, F32),
            pltpu.VMEM((line - 1,) + piece, F32),
            pltpu.VMEM((line,) + piece, F32),
            pltpu.VMEM((4, 8, 128), F32),
            pltpu.VMEM((2 + line, 8, 128), F32),
            pltpu.VMEM((COLS_OWN, 8, 128), F32),
            pltpu.VMEM((COLS_OWN, 8, 128), F32),
            pltpu.VMEM((3, 8, 128), F32),
            dma((LOADS,)),
            dma((line,)), dma((line,)),
            dma((line, 2)), dma((line, 2)),
            dma((line,)), dma((line,)),
            dma((line - 1,)), dma((line - 1,)),
            dma((line - 1,)), dma((line - 1,)),
            dma((3, line)), dma((3, line)),
            dma((PLANE, line)), dma((PLANE, line)),
            dma((2 + line,)), dma((2 + line,)),
        ],
        compiler_params=pltpu.CompilerParams(
            collective_id=0, has_side_effects=True, vmem_limit_bytes=60 * 1024 * 1024
        ),
    )(owner, block_col, block_row, codes, blocks, right_side.T)
    return (sol.T, left.T, rel[:, 0])


def solution(mesh):
    placed = (
        P(("grp", "shard"), None, None),
        P(("grp", "shard")),
        P(("grp", "shard"), None),
        P(("grp", "shard")),
        P(("grp", "shard"), None),
    )
    return jax.shard_map(
        on_device,
        mesh=mesh,
        in_specs=placed,
        out_specs=(P("shard", None), P(("grp", "shard"), None), P()),
        check_vma=False,
    )
```

time: 598 us -> 158 us (0.26); the launches traced: 591 us -> 158 us
  blocking collectives: 404 us -> 0 us
  Pallas kernels: 0 us -> 152 us
  matrix products: 68.2 us -> 0 us
  starting transfers between devices: 36.9 us -> 0 us
  waiting for transfers between devices: 29.3 us -> 0 us
  local copies, waits for them, and re-layouts: 28.3 us -> 4.52 us
  between operations: 14.6 us -> 0.66 us
  other arithmetic: 10.2 us -> 1.31 us
    psum x9 -> x0, blocking collectives: 363 us -> none  [the longest x5 194 us: norm_rows(): return jnp.sqrt(lax.psum(squares_by_column(values), ('grp', 'shard')))]
    pallas_call x0 -> x1, Pallas kernels: none -> 152 us  [on_device(): pl.pallas_call(functools.partial(kernel, shards, count, rows), out_shape=...]
    dot_general x20 -> x0, matrix products: 68.2 us -> none  [the longest x4 33.3 us: on_device(): jnp.einsum('kij,kjr->kir', blocks, forward_pieces, precision=PRECISE)]
    all_to_all x3 -> x0, blocking collectives: 40.2 us -> none  [adjoint(): lax.all_to_all(padded[source], 'shard', split_axis=0, concat_axis=0, tile...]
    all_to_all x6 -> x0, starting transfers between devices: 36.7 us -> none  [the longest x4 22.9 us: on_device(): lax.all_to_all(outgoing, 'shard', split_axis=0, concat_axis=0, tiled=True)]
    psum x4 -> x0, waiting for transfers between devices: 16.2 us -> none  [adjoint(): owned = lax.psum(owned, 'grp')]
    all_to_all x6 -> x0, waiting for transfers between devices: 13.1 us -> none  [the longest x1 13 us: adjoint(): lax.all_to_all(padded[source], 'shard', split_axis=0, concat_axis=0, tile...]
    reshape x24 -> x0, local copies, waits for them, and re-layouts: 12.1 us -> none  [the longest x8 6.87 us: adjoint(): return owned.reshape(COLS_OWN * block_width, columns)]
  transfers between devices with their start and end apart: 10 -> 0, of which waited for: 2 -> 0; matrix products, arithmetic and copies ran while one was open for 3% -> 0% of each run, Pallas kernels for 0% -> 0%
where the time goes in v1:
time: 158 us
  Pallas kernels  152 us (96%)
  local copies, waits for them, and re-layouts  4.52 us (3%)
    pallas_call x1, Pallas kernels, on_device(): pl.pallas_call(functools.partial(kernel, shards, count, rows), out_shape=...  152 us

profile of v1, /device:TPU:0, one launch (start us, length us, event | category | flops | bytes accessed | tf_op | source)
XLA Modules:
  0.0 158.1 jit_solution(12673300072345416548)
XLA Ops:
  0.6 0.7 fusion.1
  1.4 0.1 add.44
  1.5 0.1 add.41
  1.5 0.1 add.42
  1.6 0.6 broadcast_add_fusion.code_ref
  2.2 151.7 %shard_map.76 = (f32[8,2048]{1,0:T(8,128)}, f32[8,2048]{1,0:T(8,128)}, f32[8,128]{1,0:T(8,128)}) custom-call(s32[64]{0:T(128)} %bitcast.12, s32[64]{0:T(128)} %col_ref.1, s32[64]{0:T(128)} %row_ref.1, s32[2,512]{1,0:T(2,128)} %broadcast_add_fusion.code_ref, f32[64,128,128]{2,1,0:T(8,128)} %blocks_ref.1, f32[8,2048]{1,0:T(8,128)} %bitcast.9), custom_call_target="tpu_custom_call" | custom-call | tf_op jit(solution)/shard_map/pallas_call | solution.py:374
  153.9 1.3 slice_reduce_fusion
  155.2 1.5 copy.10
  156.7 1.5 copy.11
  (2 shorter events, 0.0 us)

commit v2 on v1

--- a/solution.py
+++ b/solution.py
@@ -12,6 +12,7 @@
 HALF = COLS_OWN // 2
 PLANE = 4
 LOADS = 8
+GROUP = 32
 MESH = pl.DeviceIdType.MESH
 F32 = jnp.float32
 BF16 = jnp.bfloat16
@@ -31,9 +32,9 @@
     owner_ref, col_ref, row_ref, code_ref, blocks_ref, right_ref,
     sol_ref, left_out, rel_ref,
     raw, pair, scatter, gather_rows, prod, left, unit, image,
-    full, part, cross, from_a, from_b, relay, from_z, to_z, norms, norms_in,
+    full, part, cross, from_a, from_z, to_z, norms, norms_in,
     own, search, bidiag,
-    load_sem, x_send, x_recv, a_send, a_recv, b_send, b_recv, c_send, c_recv,
+    load_sem, x_send, x_recv, a_send, a_recv, c_send, c_recv,
     z_send, z_recv, p_send, p_recv, g_send, g_recv, n_send, n_recv,
 ):
     line = shards // PLANE
@@ -41,20 +42,20 @@
     me = lax.axis_index("shard")
     high, low = me // PLANE, me % PLANE
 
-    def flip(d):
-        bit0 = low % 2
-        bit1 = low // 2
-        if d & 1:
-            bit0 = 1 - bit0
-        if d & 2:
-            bit1 = 1 - bit1
-        return bit1 * 2 + bit0
-
-    lows = [flip(d) for d in range(PLANE)]
-    ahead = [lax.rem(high + e, line) for e in range(line)]
-    behind = [lax.rem(high + line - e, line) for e in range(line)]
+    def flip(index, d, size):
+        out, weight = 0, 1
+        while weight < size:
+            bit = (index // weight) % 2
+            if d & weight:
+                bit = 1 - bit
+            out = out + bit * weight
+            weight *= 2
+        return out
+
+    lows = [flip(low, d, PLANE) for d in range(PLANE)]
+    ahead = [flip(high, e, line) for e in range(line)]
     partner = (1 - grp, me)
-    plane = {d: (grp, high * PLANE + lows[d]) for d in (1, 2)}
+    plane = {d: (grp, high * PLANE + lows[d]) for d in (1, 2, 3)}
     along = {e: (grp, ahead[e] * PLANE + low) for e in range(1, line)}
 
     def remote(src, dst, send, recv, device):
@@ -76,7 +77,7 @@
         copy.start()
 
     barrier = pltpu.get_barrier_semaphore()
-    greeted = [partner, plane[1], plane[2]] + [along[e] for e in range(1, line)]
+    greeted = [partner, plane[1], plane[2], plane[3]] + [along[e] for e in range(1, line)]
     for device in greeted:
         pl.semaphore_signal(barrier, inc=1, device_id=device, device_id_type=MESH)
 
@@ -131,8 +132,8 @@
 
     def adjoint(step, carry):
         tiles = []
-        for i in range(4):
-            k = step * 4 + i
+        for i in range(GROUP):
+            k = step * GROUP + i
             out = jnp.dot(both(left[row_ref[k] % rows]), pair[k], preferred_element_type=F32)
             out = out[:, 0:128] + out[:, 128:256]
             tiles.append(out[0:8] + out[8:16])
@@ -141,8 +142,8 @@
 
     def forward(step, carry):
         tiles = []
-        for i in range(4):
-            k = step * 4 + i
+        for i in range(GROUP):
+            k = step * GROUP + i
             col = col_ref[k]
             tile = full[(col // HALF) * shards + owner_ref[k], col % HALF]
             lhs = both(tile)
@@ -166,7 +167,7 @@
     def reduce_scatter():
         sends = []
         columns_of(1 - grp)
-        order = [e for e in range(1, line)] + [0]
+        order = list(range(line - 1, -1, -1))
         exchange = {}
         for e in order:
             first = ahead[e] * PLANE
@@ -184,29 +185,20 @@
             cross[pl.ds(first, PLANE)] = (
                 cross[pl.ds(first, PLANE)] + part[pl.ds(grp * shards + first, PLANE)]
             )
-            a = 1 if e % 2 == 0 else 2
-            for i, d in enumerate((3, a)):
+            for d in (1, 2, 3):
                 copy = remote(
-                    cross.at[first + lows[d]], from_a.at[e, i],
-                    a_send.at[e, i], a_recv.at[e, i], plane[a],
+                    cross.at[first + lows[d]], from_a.at[e, d - 1],
+                    a_send.at[e, d - 1], a_recv.at[e, d - 1], plane[d],
                 )
                 copy.start()
-                stage_a[e, i] = copy
-        stage_b = {}
-        for e in order:
-            first = ahead[e] * PLANE
-            b = 2 if e % 2 == 0 else 1
-            stage_a[e, 0].wait_recv()
-            relay[e] = cross[first + lows[b]] + from_a[e, 0]
-            stage_b[e] = remote(relay.at[e], from_b.at[e], b_send.at[e], b_recv.at[e], plane[b])
-            stage_b[e].start()
+                stage_a[e, d] = copy
         stage_c = {}
         for e in order:
-            first = ahead[e] * PLANE
-            stage_a[e, 1].wait_recv()
-            mine = cross[first + low] + from_a[e, 1]
-            stage_b[e].wait_recv()
-            to_z[e] = mine + from_b[e]
+            mine = cross[ahead[e] * PLANE + low]
+            for d in (1, 2, 3):
+                stage_a[e, d].wait_recv()
+                mine = mine + from_a[e, d - 1]
+            to_z[e] = mine
             if e:
                 stage_c[e] = remote(
                     to_z.at[e], from_z.at[e - 1], c_send.at[e - 1], c_recv.at[e - 1], along[e]
@@ -217,13 +209,13 @@
         summed = to_z[0]
         for e in range(1, line):
             summed = summed + from_z[e - 1]
-        for copies in (exchange, stage_a, stage_b, stage_c):
+        for copies in (exchange, stage_a, stage_c):
             for copy in copies.values():
                 copy.wait_send()
         return summed
 
     def slot(e, d):
-        return grp * shards + behind[e] * PLANE + lows[d]
+        return grp * shards + ahead[e] * PLANE + lows[d]
 
     def all_gather():
         sends = []
@@ -238,7 +230,7 @@
             sends.append(copy)
 
         def spread(e):
-            for d in (1, 2):
+            for d in (1, 2, 3):
                 copy = piece(e, 0, p_send.at[d - 1, e], p_recv.at[d - 1, e], plane[d])
                 copy.start()
                 sends.append(copy)
@@ -252,30 +244,18 @@
         def arrive(e, d):
             piece(e, d, p_send.at[d - 1, e], p_recv.at[d - 1, e], plane[1]).wait_recv()
 
-        def pass_on(e):
-            a = 1 if e % 2 == 0 else 2
-            b = 3 - a
-            arrive(e, a)
-            copy = piece(e, a, p_send.at[2, e], p_recv.at[2, e], plane[b])
-            copy.start()
-            sends.append(copy)
-            hand(e, a)
-            arrive(e, b)
-            hand(e, b)
-
         spread(0)
         for e in range(1, line):
             piece(e, 0, z_send.at[e - 1], z_recv.at[e - 1], along[e]).wait_recv()
             spread(e)
-            pass_on(e - 1)
-        pass_on(line - 1)
         for e in range(line):
-            arrive(e, 3)
-            hand(e, 3)
+            for d in (1, 2, 3):
+                arrive(e, d)
+                hand(e, d)
         other = (1 - grp) * shards
         for e in range(line):
             for d in range(PLANE):
-                place = full.at[other + behind[e] * PLANE + lows[d]]
+                place = full.at[other + ahead[e] * PLANE + lows[d]]
                 remote(place, place, g_send.at[d, e], g_recv.at[d, e], partner).wait_recv()
         for copy in sends:
             copy.wait_send()
@@ -297,7 +277,7 @@
     bidiag[1] = jnp.zeros((8, 128), F32)
 
     def iterate(it, carry):
-        lax.fori_loop(0, count // 4, adjoint, 0)
+        lax.fori_loop(0, count // GROUP, adjoint, 0)
         summed = reduce_scatter()
         norm_left = jnp.sqrt(total(summed[HALF]))
         squares = jnp.zeros((8, 128), F32)
@@ -320,7 +300,7 @@
         bidiag[0] = jnp.where(it == 0, norm_right, -cosine * norm_right)
         bidiag[1] = jnp.where(it == 0, norm_left, sine * residual)
         bidiag[2] = jnp.where(it == 0, norm_left, bidiag[2])
-        lax.fori_loop(0, count // 4, forward, 0)
+        lax.fori_loop(0, count // GROUP, forward, 0)
         out = jnp.dot(gather_rows[...], prod[...], preferred_element_type=F32)
         out = (out[:, 0:128] + out[:, 128:256]).reshape(rows, 8, 128)
         fresh = out / norm_right[None] - norm_right[None] * (left[...] / norm_left[None])
@@ -331,23 +311,24 @@
     bidiag[2] = jnp.zeros((8, 128), F32)
     lax.fori_loop(0, ITERS, iterate, 0)
 
+    def swap(i, first, devices):
+        copies = [
+            remote(norms.at[i], norms_in.at[first + x], n_send.at[first + x], n_recv.at[first + x], y)
+            for x, y in enumerate(devices)
+        ]
+        for copy in copies:
+            copy.start()
+        summed = norms[i]
+        for x, copy in enumerate(copies):
+            copy.wait_recv()
+            summed = summed + norms_in[first + x]
+        sent.extend(copies)
+        return summed
+
     sent = []
-    for i, device in enumerate((partner, plane[1], plane[2])):
-        copy = remote(norms.at[i], norms_in.at[i], n_send.at[i], n_recv.at[i], device)
-        copy.start()
-        copy.wait_recv()
-        norms[i + 1] = norms[i] + norms_in[i]
-        sent.append(copy)
-    summed = norms[3]
-    for e in range(1, line):
-        copy = remote(
-            norms.at[3], norms_in.at[2 + e], n_send.at[2 + e], n_recv.at[2 + e], along[e]
-        )
-        copy.start()
-        sent.append(copy)
-    for e in range(1, line):
-        sent[2 + e].wait_recv()
-        summed = summed + norms_in[2 + e]
+    norms[1] = swap(0, 0, [partner])
+    norms[2] = swap(1, 1, [plane[d] for d in (1, 2, 3)])
+    summed = swap(2, 4, [along[e] for e in range(1, line)])
     norm_left = jnp.sqrt(total(summed))
     radius, cosine, sine, residual = rotation(norm_left)
     advance(radius, cosine, residual)
@@ -392,25 +373,22 @@
             pltpu.VMEM((2 * shards,) + piece, F32),
             pltpu.VMEM((2 * shards,) + piece, F32),
             pltpu.VMEM((shards,) + piece, F32),
-            pltpu.VMEM((line, 2) + piece, F32),
-            pltpu.VMEM((line,) + piece, F32),
-            pltpu.VMEM((line,) + piece, F32),
+            pltpu.VMEM((line, 3) + piece, F32),
             pltpu.VMEM((line - 1,) + piece, F32),
             pltpu.VMEM((line,) + piece, F32),
-            pltpu.VMEM((4, 8, 128), F32),
-            pltpu.VMEM((2 + line, 8, 128), F32),
+            pltpu.VMEM((3, 8, 128), F32),
+            pltpu.VMEM((3 + line, 8, 128), F32),
             pltpu.VMEM((COLS_OWN, 8, 128), F32),
             pltpu.VMEM((COLS_OWN, 8, 128), F32),
             pltpu.VMEM((3, 8, 128), F32),
             dma((LOADS,)),
             dma((line,)), dma((line,)),
-            dma((line, 2)), dma((line, 2)),
-            dma((line,)), dma((line,)),
+            dma((line, 3)), dma((line, 3)),
             dma((line - 1,)), dma((line - 1,)),
             dma((line - 1,)), dma((line - 1,)),
             dma((3, line)), dma((3, line)),
             dma((PLANE, line)), dma((PLANE, line)),
-            dma((2 + line,)), dma((2 + line,)),
+            dma((3 + line,)), dma((3 + line,)),
         ],
         compiler_params=pltpu.CompilerParams(
             collective_id=0, has_side_effects=True, vmem_limit_bytes=60 * 1024 * 1024

time: 158 us -> 123 us (0.78)
  Pallas kernels: 152 us -> 116 us
    pallas_call x1, Pallas kernels: 152 us -> 116 us  [on_device(): pl.pallas_call(functools.partial(kernel, shards, count, rows), out_shape=...]
where the time goes in v2:
time: 123 us
  Pallas kernels  116 us (94%)
  local copies, waits for them, and re-layouts  4.52 us (4%)
  other arithmetic  1.31 us (1%)
    pallas_call x1, Pallas kernels, on_device(): pl.pallas_call(functools.partial(kernel, shards, count, rows), out_shape=...  116 us
    unnamed x2, local copies, waits for them, and re-layouts  2.94 us

profile of v2, /device:TPU:0, one launch (start us, length us, event | category | flops | bytes accessed | tf_op | source)
XLA Modules:
  0.0 123.0 jit_solution(12455055771138571953)
XLA Ops:
  0.6 0.7 fusion.1
  1.4 0.1 add.44
  1.5 0.1 add.41
  1.5 0.1 add.42
  1.6 0.6 broadcast_add_fusion.code_ref
  2.2 116.5 %shard_map.76 = (f32[8,2048]{1,0:T(8,128)}, f32[8,2048]{1,0:T(8,128)}, f32[8,128]{1,0:T(8,128)}) custom-call(s32[64]{0:T(128)} %bitcast.12, s32[64]{0:T(128)} %col_ref.1, s32[64]{0:T(128)} %row_ref.1, s32[2,512]{1,0:T(2,128)} %broadcast_add_fusion.code_ref, f32[64,128,128]{2,1,0:T(8,128)} %blocks_ref.1, f32[8,2048]{1,0:T(8,128)} %bitcast.9), custom_call_target="tpu_custom_call" | custom-call | tf_op jit(solution)/shard_map/pallas_call | solution.py:355
  118.7 1.3 %slice_reduce_fusion = f32[8]{0:T(128)} fusion(f32[8,128]{1,0:T(8,128)} %get-tuple-element.8), kind=kLoop, calls=%fused_computation | loop fusion | bytes 64 | tf_op jit(solution)/shard_map/slice | solution.py:397
  120.0 1.5 %copy.10 = f32[2048,8]{0,1:T(8,128)} copy(f32[2048,8]{0,1:T(8,128)} %bitcast.11) | data formatting | bytes 131072
  121.5 1.5 %copy.11 = f32[2048,8]{0,1:T(8,128)} copy(f32[2048,8]{0,1:T(8,128)} %bitcast.10) | data formatting | bytes 131072
  (2 shorter events, 0.0 us)

commit v3 on v2

--- a/solution.py
+++ b/solution.py
@@ -29,10 +29,10 @@
 
 def kernel(
     shards, count, rows,
-    owner_ref, col_ref, row_ref, code_ref, blocks_ref, right_ref,
+    owner_ref, col_ref, row_ref, blocks_ref, right_ref,
     sol_ref, left_out, rel_ref,
     raw, pair, scatter, gather_rows, prod, left, unit, image,
-    full, part, cross, from_a, from_z, to_z, norms, norms_in,
+    full, part, cross, from_a, from_z, to_z, norms, norms_in, partial,
     own, search, bidiag,
     load_sem, x_send, x_recv, a_send, a_recv, c_send, c_recv,
     z_send, z_recv, p_send, p_recv, g_send, g_recv, n_send, n_recv,
@@ -86,10 +86,25 @@
         tile = right_ref[:, r * 128:(r + 1) * 128]
         left[r] = tile
         squares = squares + tile * tile
-    norms[0] = squares
-
-    codes = code_ref[0:1, :]
-    row_codes = code_ref[1:2, :]
+    partial[...] = squares
+
+    lanes = lax.broadcasted_iota(jnp.int32, (8, count * 8), 1)
+
+    def code(k, carry):
+        codes, row_codes = carry
+        col = col_ref[k]
+        place = ((col // HALF) * shards + owner_ref[k]) * HALF + col % HALF
+        here = (lanes >= k * 8) & (lanes < k * 8 + 8)
+        shift = lanes - k * 8
+        return (
+            jnp.where(here, place * 8 + shift, codes),
+            jnp.where(here, (row_ref[k] % rows) * 8 + shift, row_codes),
+        )
+
+    codes, row_codes = lax.fori_loop(
+        0, count, code, (jnp.zeros_like(lanes), jnp.zeros_like(lanes)), unroll=4
+    )
+    codes, row_codes = codes[0:1], row_codes[0:1]
     ids = lax.broadcasted_iota(jnp.int32, (HALF * 8, count * 8), 0)
 
     def build(q, carry):
@@ -161,11 +176,34 @@
             lhs = scatter[pl.ds(base, 16)].reshape(16 * HALF * 8, count * 8)
             out = jnp.dot(lhs, prod[...], preferred_element_type=F32)
             out = out[:, 0:128] + out[:, 128:256]
-            part[pl.ds(base, 16), 0:HALF] = out.reshape(16, HALF, 8, 128)
-            part[pl.ds(base, 16), HALF] = jnp.broadcast_to(norms[0][None], (16, 8, 128))
-
-    def reduce_scatter():
-        sends = []
+            part[pl.ds(base, 16)] = out.reshape(16, HALF, 8, 128)
+
+    def norm_exchange(kind, summed):
+        sent = []
+        first = 0
+        hops = ([partner], [plane[d] for d in (1, 2, 3)], [along[e] for e in range(1, line)])
+        for stage, devices in enumerate(hops):
+            norms[kind, stage] = summed
+            copies = []
+            for x, device in enumerate(devices):
+                at = first + x
+                copies.append(remote(
+                    norms.at[kind, stage], norms_in.at[kind, at],
+                    n_send.at[kind, at], n_recv.at[kind, at], device,
+                ))
+                copies[-1].start()
+            yield None
+            for x, copy in enumerate(copies):
+                copy.wait_recv()
+                summed = summed + norms_in[kind, first + x]
+            first += len(devices)
+            sent += copies
+        for copy in sent:
+            copy.wait_send()
+        yield summed
+
+    def reduce_scatter(ends):
+        next(ends)
         columns_of(1 - grp)
         order = list(range(line - 1, -1, -1))
         exchange = {}
@@ -192,6 +230,7 @@
                 )
                 copy.start()
                 stage_a[e, d] = copy
+        next(ends)
         stage_c = {}
         for e in order:
             mine = cross[ahead[e] * PLANE + low]
@@ -212,12 +251,13 @@
         for copies in (exchange, stage_a, stage_c):
             for copy in copies.values():
                 copy.wait_send()
-        return summed
+        return summed, next(ends)
 
     def slot(e, d):
         return grp * shards + ahead[e] * PLANE + lows[d]
 
-    def all_gather():
+    def all_gather(ends):
+        next(ends)
         sends = []
 
         def piece(e, d, send, recv, device):
@@ -248,6 +288,9 @@
         for e in range(1, line):
             piece(e, 0, z_send.at[e - 1], z_recv.at[e - 1], along[e]).wait_recv()
             spread(e)
+            if e == 1:
+                next(ends)
+        next(ends)
         for e in range(line):
             for d in (1, 2, 3):
                 arrive(e, d)
@@ -259,6 +302,7 @@
                 remote(place, place, g_send.at[d, e], g_recv.at[d, e], partner).wait_recv()
         for copy in sends:
             copy.wait_send()
+        return next(ends)
 
     def rotation(norm_left):
         diag_bar, residual = bidiag[0], bidiag[1]
@@ -277,22 +321,22 @@
     bidiag[1] = jnp.zeros((8, 128), F32)
 
     def iterate(it, carry):
+        ends = norm_exchange(0, partial[...])
+        next(ends)
         lax.fori_loop(0, count // GROUP, adjoint, 0)
-        summed = reduce_scatter()
-        norm_left = jnp.sqrt(total(summed[HALF]))
-        squares = jnp.zeros((8, 128), F32)
+        summed, squares = reduce_scatter(ends)
+        norm_left = jnp.sqrt(total(squares))
         mine = slot(0, 0)
         previous = own[pl.ds(grp * HALF, HALF)]
-        fresh = summed[0:HALF] / norm_left[None] - norm_left[None] * previous
-        full[mine, 0:HALF] = fresh
-        full[mine, HALF] = jnp.sum(fresh * fresh, axis=0)
-        all_gather()
-        norm_right = jnp.sqrt(total(jnp.sum(full[:, HALF], axis=0)))
+        fresh = summed / norm_left[None] - norm_left[None] * previous
+        full[mine] = fresh
+        squares = all_gather(norm_exchange(1, jnp.sum(fresh * fresh, axis=0)))
+        norm_right = jnp.sqrt(total(squares))
         radius, cosine, sine, residual = rotation(norm_left)
         advance(radius, cosine, residual)
         shrink = sine * norm_right / radius
         for half in range(2):
-            fresh = full[half * shards + me, 0:HALF] / norm_right[None]
+            fresh = full[half * shards + me] / norm_right[None]
             own[half * HALF:(half + 1) * HALF] = fresh
             search[half * HALF:(half + 1) * HALF] = (
                 fresh - shrink[None] * search[half * HALF:(half + 1) * HALF]
@@ -305,38 +349,22 @@
         out = (out[:, 0:128] + out[:, 128:256]).reshape(rows, 8, 128)
         fresh = out / norm_right[None] - norm_right[None] * (left[...] / norm_left[None])
         left[...] = fresh
-        norms[0] = jnp.sum(fresh * fresh, axis=0)
+        partial[...] = jnp.sum(fresh * fresh, axis=0)
         return carry
 
     bidiag[2] = jnp.zeros((8, 128), F32)
     lax.fori_loop(0, ITERS, iterate, 0)
 
-    def swap(i, first, devices):
-        copies = [
-            remote(norms.at[i], norms_in.at[first + x], n_send.at[first + x], n_recv.at[first + x], y)
-            for x, y in enumerate(devices)
-        ]
-        for copy in copies:
-            copy.start()
-        summed = norms[i]
-        for x, copy in enumerate(copies):
-            copy.wait_recv()
-            summed = summed + norms_in[first + x]
-        sent.extend(copies)
-        return summed
-
-    sent = []
-    norms[1] = swap(0, 0, [partner])
-    norms[2] = swap(1, 1, [plane[d] for d in (1, 2, 3)])
-    summed = swap(2, 4, [along[e] for e in range(1, line)])
+    ends = norm_exchange(0, partial[...])
+    for _ in range(3):
+        next(ends)
+    summed = next(ends)
     norm_left = jnp.sqrt(total(summed))
     radius, cosine, sine, residual = rotation(norm_left)
     advance(radius, cosine, residual)
     for r in range(rows):
         left_out[:, r * 128:(r + 1) * 128] = left[r] / norm_left
     rel_ref[...] = sine * residual / bidiag[2]
-    for copy in sent:
-        copy.wait_send()
 
 
 def on_device(blocks, block_row, block_owner, block_col, right_side):
@@ -345,10 +373,7 @@
     shards = lax.axis_size("shard")
     line = shards // PLANE
     owner = block_owner[:, 0]
-    place = ((block_col // HALF) * shards + owner) * HALF + block_col % HALF
-    both = jnp.stack([place, block_row % rows])
-    codes = (both[:, :, None] * 8 + jnp.arange(8, dtype=jnp.int32)).reshape(2, count * 8)
-    piece = (HALF + 1, 8, 128)
+    piece = (HALF, 8, 128)
     smem = pl.BlockSpec(memory_space=pltpu.SMEM)
     vmem = pl.BlockSpec(memory_space=pltpu.VMEM)
     dma = pltpu.SemaphoreType.DMA
@@ -359,7 +384,7 @@
             jax.ShapeDtypeStruct((8, rows * 128), F32),
             jax.ShapeDtypeStruct((8, 128), F32),
         ),
-        in_specs=[smem, smem, smem, vmem, pl.BlockSpec(memory_space=pl.ANY), vmem],
+        in_specs=[smem, smem, smem, pl.BlockSpec(memory_space=pl.ANY), vmem],
         out_specs=(vmem, vmem, vmem),
         scratch_shapes=[
             pltpu.VMEM((count, 128, 128), F32),
@@ -376,8 +401,9 @@
             pltpu.VMEM((line, 3) + piece, F32),
             pltpu.VMEM((line - 1,) + piece, F32),
             pltpu.VMEM((line,) + piece, F32),
-            pltpu.VMEM((3, 8, 128), F32),
-            pltpu.VMEM((3 + line, 8, 128), F32),
+            pltpu.VMEM((2, 3, 8, 128), F32),
+            pltpu.VMEM((2, 3 + line, 8, 128), F32),
+            pltpu.VMEM((8, 128), F32),
             pltpu.VMEM((COLS_OWN, 8, 128), F32),
             pltpu.VMEM((COLS_OWN, 8, 128), F32),
             pltpu.VMEM((3, 8, 128), F32),
@@ -388,12 +414,12 @@
             dma((line - 1,)), dma((line - 1,)),
             dma((3, line)), dma((3, line)),
             dma((PLANE, line)), dma((PLANE, line)),
-            dma((3 + line,)), dma((3 + line,)),
+            dma((2, 3 + line)), dma((2, 3 + line)),
         ],
         compiler_params=pltpu.CompilerParams(
             collective_id=0, has_side_effects=True, vmem_limit_bytes=60 * 1024 * 1024
         ),
-    )(owner, block_col, block_row, codes, blocks, right_side.T)
+    )(owner, block_col, block_row, blocks, right_side.T)
     return (sol.T, left.T, rel[:, 0])
 
 

time: 123 us -> 122 us (level)
  other arithmetic: 1.31 us -> 0 us
where the time goes in v3:
time: 122 us
  Pallas kernels  117 us (96%)
  local copies, waits for them, and re-layouts  4.24 us (3%)
    pallas_call x1, Pallas kernels, on_device(): pl.pallas_call(functools.partial(kernel, shards, count, rows), out_shape=...  117 us
    unnamed x2, local copies, waits for them, and re-layouts  2.94 us

profile of v3, /device:TPU:0, one launch (start us, length us, event | category | flops | bytes accessed | tf_op | source)
XLA Modules:
  0.0 122.0 jit_solution(14170824542747996428)
XLA Ops:
  0.6 117.1 %shard_map.76 = (f32[8,2048]{1,0:T(8,128)}, f32[8,2048]{1,0:T(8,128)}, f32[8,128]{1,0:T(8,128)}) custom-call(s32[64]{0:T(128)} %bitcast.7, s32[64]{0:T(128)} %col_ref.1, s32[64]{0:T(128)} %row_ref.1, f32[64,128,128]{2,1,0:T(8,128)} %blocks_ref.1, f32[8,2048]{1,0:T(8,128)} %bitcast.4), custom_call_target="tpu_custom_call" | custom-call | tf_op jit(solution)/shard_map/pallas_call | solution.py:380
  117.8 1.3 %slice_reduce_fusion = f32[8]{0:T(128)} fusion(f32[8,128]{1,0:T(8,128)} %get-tuple-element.8), kind=kLoop, calls=%fused_computation | loop fusion | bytes 64 | tf_op jit(solution)/shard_map/slice | solution.py:423
  119.1 1.5 %copy.10 = f32[2048,8]{0,1:T(8,128)} copy(f32[2048,8]{0,1:T(8,128)} %bitcast.6) | data formatting | bytes 131072
  120.5 1.5 %copy.11 = f32[2048,8]{0,1:T(8,128)} copy(f32[2048,8]{0,1:T(8,128)} %bitcast.5) | data formatting | bytes 131072

commit v4 on v3

--- a/solution.py
+++ b/solution.py
@@ -56,6 +56,7 @@
     ahead = [flip(high, e, line) for e in range(line)]
     partner = (1 - grp, me)
     plane = {d: (grp, high * PLANE + lows[d]) for d in (1, 2, 3)}
+    slant = [(1 - grp, high * PLANE + lows[d]) for d in (1, 2, 3)]
     along = {e: (grp, ahead[e] * PLANE + low) for e in range(1, line)}
 
     def remote(src, dst, send, recv, device):
@@ -77,7 +78,7 @@
         copy.start()
 
     barrier = pltpu.get_barrier_semaphore()
-    greeted = [partner, plane[1], plane[2], plane[3]] + [along[e] for e in range(1, line)]
+    greeted = [partner, plane[1], plane[2], plane[3]] + slant + [along[e] for e in range(1, line)]
     for device in greeted:
         pl.semaphore_signal(barrier, inc=1, device_id=device, device_id_type=MESH)
 
@@ -181,7 +182,10 @@
     def norm_exchange(kind, summed):
         sent = []
         first = 0
-        hops = ([partner], [plane[d] for d in (1, 2, 3)], [along[e] for e in range(1, line)])
+        hops = (
+            [partner] + [plane[d] for d in (1, 2, 3)] + slant,
+            [along[e] for e in range(1, line)],
+        )
         for stage, devices in enumerate(hops):
             norms[kind, stage] = summed
             copies = []
@@ -203,7 +207,6 @@
         yield summed
 
     def reduce_scatter(ends):
-        next(ends)
         columns_of(1 - grp)
         order = list(range(line - 1, -1, -1))
         exchange = {}
@@ -290,7 +293,6 @@
             spread(e)
             if e == 1:
                 next(ends)
-        next(ends)
         for e in range(line):
             for d in (1, 2, 3):
                 arrive(e, d)
@@ -356,7 +358,7 @@
     lax.fori_loop(0, ITERS, iterate, 0)
 
     ends = norm_exchange(0, partial[...])
-    for _ in range(3):
+    for _ in range(2):
         next(ends)
     summed = next(ends)
     norm_left = jnp.sqrt(total(summed))
@@ -401,8 +403,8 @@
             pltpu.VMEM((line, 3) + piece, F32),
             pltpu.VMEM((line - 1,) + piece, F32),
             pltpu.VMEM((line,) + piece, F32),
-            pltpu.VMEM((2, 3, 8, 128), F32),
-            pltpu.VMEM((2, 3 + line, 8, 128), F32),
+            pltpu.VMEM((2, 2, 8, 128), F32),
+            pltpu.VMEM((2, 6 + line, 8, 128), F32),
             pltpu.VMEM((8, 128), F32),
             pltpu.VMEM((COLS_OWN, 8, 128), F32),
             pltpu.VMEM((COLS_OWN, 8, 128), F32),
@@ -414,7 +416,7 @@
             dma((line - 1,)), dma((line - 1,)),
             dma((3, line)), dma((3, line)),
             dma((PLANE, line)), dma((PLANE, line)),
-            dma((2, 3 + line)), dma((2, 3 + line)),
+            dma((2, 6 + line)), dma((2, 6 + line)),
         ],
         compiler_params=pltpu.CompilerParams(
             collective_id=0, has_side_effects=True, vmem_limit_bytes=60 * 1024 * 1024

time: 122 us -> 119 us (0.975)
  Pallas kernels: 117 us -> 114 us
    pallas_call x1, Pallas kernels: 117 us -> 114 us  [on_device(): pl.pallas_call(functools.partial(kernel, shards, count, rows), out_shape=...]
where the time goes in v4:
time: 119 us
  Pallas kernels  114 us (96%)
  local copies, waits for them, and re-layouts  4.24 us (4%)
    pallas_call x1, Pallas kernels, on_device(): pl.pallas_call(functools.partial(kernel, shards, count, rows), out_shape=...  114 us
    unnamed x2, local copies, waits for them, and re-layouts  2.94 us

profile of v4, /device:TPU:0, one launch (start us, length us, event | category | flops | bytes accessed | tf_op | source)
XLA Modules:
  0.0 118.7 jit_solution(14129912825155389443)
XLA Ops:
  0.6 113.8 %shard_map.76 = (f32[8,2048]{1,0:T(8,128)}, f32[8,2048]{1,0:T(8,128)}, f32[8,128]{1,0:T(8,128)}) custom-call(s32[64]{0:T(128)} %bitcast.7, s32[64]{0:T(128)} %col_ref.1, s32[64]{0:T(128)} %row_ref.1, f32[64,128,128]{2,1,0:T(8,128)} %blocks_ref.1, f32[8,2048]{1,0:T(8,128)} %bitcast.4), custom_call_target="tpu_custom_call" | custom-call | tf_op jit(solution)/shard_map/pallas_call | solution.py:382
  114.5 1.3 %slice_reduce_fusion = f32[8]{0:T(128)} fusion(f32[8,128]{1,0:T(8,128)} %get-tuple-element.8), kind=kLoop, calls=%fused_computation | loop fusion | bytes 64 | tf_op jit(solution)/shard_map/slice | solution.py:425
  115.8 1.5 %copy.10 = f32[2048,8]{0,1:T(8,128)} copy(f32[2048,8]{0,1:T(8,128)} %bitcast.6) | data formatting | bytes 131072
  117.2 1.5 %copy.11 = f32[2048,8]{0,1:T(8,128)} copy(f32[2048,8]{0,1:T(8,128)} %bitcast.5) | data formatting | bytes 131072
